TPU v7x, 32 devices: a whole 2x2x4 slice. The times are simulated.
32 devices in a mesh: seq: 8 (over z, y), grp: 4 (over x, core).
Axes of the slice: x: 2, y: 2, z: 4, core: 2. Of those that a mesh axis runs over, the one named last changes fastest.
Arguments:
- hidden: bfloat16 [256, 8192], P('grp', 'seq'), may hold values from -6 to 6
- w_qkv: bfloat16 [8192, 10240], P('seq', 'grp'), may hold values from -0.0625 to 0.0625
- b_qkv: float32 [10240], P('grp'), may hold values from -3 to 3
- w_out: bfloat16 [8192, 8192], P('seq', 'grp'), may hold values from -0.0625 to 0.0625
- k_cache: bfloat16 [4, 32768, 1024], P('grp', 'seq'), may hold values from -600 to 600
- v_cache: bfloat16 [4, 32768, 1024], P('grp', 'seq'), may hold values from -6 to 6
- lengths: int32 [256], replicated, may hold values from 1 to 16384, as said below
- page_table: int32 [256, 128], replicated, may hold values from -1 to 255, as said below
- positions: int32 [3, 256], replicated, may hold values from 0 to 4095
- group_of: int32 [256], replicated, may hold values from 0 to 3, as said below
Outputs:
- mixed: bfloat16 [256, 8192], P('seq', 'grp')
Inputs may be any that keep to these rules, and one draw needn't show every extreme that they name: `group_of`: each group serves exactly 64 requests. `lengths`: each group has a request of exactly 16384 cached positions. `page_table`: entry j of row r is the page of request r's group pool (page p lies on that group's device p // 32 of seq) that holds its positions j * 128 to (j + 1) * 128 - 1, for j < ceil(lengths[r] / 128); later entries are -1; no page belongs to two requests.
All inputs are finite; a program needn't handle non-finite values.
Results may differ from a plain program's by a relative error of at most 0.015.
The roundings to bfloat16 on the way count: a program that leaves them out, or rounds other values in their place, can miss the bound.
Values may be sent and summed in bfloat16 or wider, within the bound.
A program may use at most 128 MiB of HBM per device.

v0:
```python
import math

import jax
import jax.numpy as jnp
from jax import lax
from jax.sharding import PartitionSpec as P

HQ = 64
KVH = 8
HD = 128
PAGE = 128


rope_base = 1000000.0
neg_fill = -1e30


def rotate_heads(values, places, col_start, head_dim, turned):
    row_count, col_count = values.shape
    columns = col_start + jnp.arange(col_count, dtype=jnp.int32)
    within = columns % head_dim
    freq_index = within % (head_dim // 2)
    inverse_freq = jnp.exp(freq_index.astype(jnp.float32) * (-2.0 * math.log(rope_base) / head_dim))
    section = jnp.where(
        freq_index < head_dim // 8,
        0,
        jnp.where(freq_index < head_dim // 8 + 3 * head_dim // 16, 1, 2),
    )
    place_float = places.astype(jnp.float32)
    chosen = jnp.where(
        section[None, :] == 0,
        place_float[0][:, None],
        jnp.where(section[None, :] == 1, place_float[1][:, None], place_float[2][:, None]),
    )
    angles = chosen * inverse_freq[None, :]
    halves = values.reshape(row_count, col_count // head_dim, 2, head_dim // 2)
    partner = jnp.concatenate([-halves[:, :, 1:], halves[:, :, :1]], axis=2).reshape(
        row_count, col_count
    )
    rotated = values * jnp.cos(angles) + partner * jnp.sin(angles)
    return jnp.where((columns < turned)[None, :], rotated, values)


def shards(hidden, w_qkv, b_qkv, w_out, k_cache, v_cache, lengths, page_table, positions, group_of):
    seq_count = lax.axis_size("seq")
    grp_count = lax.axis_size("grp")
    seq_index = lax.axis_index("seq")
    grp_index = lax.axis_index("grp")
    request_total = group_of.shape[0]
    group_size = request_total // grp_count
    col_count = w_qkv.shape[1]
    col_start = grp_index * col_count
    turned = (HQ + KVH) * HD
    group_q = HQ // KVH
    score_scale = HD ** (-0.5)
    partial_sum = jnp.dot(
        lax.all_gather(hidden, "grp", axis=0, tiled=True), w_qkv, preferred_element_type=jnp.float32
    )
    request_ids = jnp.arange(request_total, dtype=jnp.int32)
    before = (group_of[None, :] < group_of[:, None]) | (group_of[None, :] == group_of[:, None]) & (
        request_ids[None, :] < request_ids[:, None]
    )
    restore = jnp.sum(before.astype(jnp.int32), axis=1)
    placed_at = restore[None, :] == request_ids[:, None]
    served_order = jnp.sum(jnp.where(placed_at, request_ids[None, :], 0), axis=1)
    served_ids = lax.dynamic_slice_in_dim(served_order, grp_index * group_size, group_size, 0)
    summed = lax.psum(partial_sum, "seq")
    fresh_rows = rotate_heads(summed + b_qkv[None, :], positions, col_start, HD, turned).astype(
        jnp.bfloat16
    )
    outgoing = fresh_rows[served_order].reshape(grp_count, group_size, col_count)
    incoming = lax.all_to_all(outgoing, "grp", split_axis=0, concat_axis=2, tiled=True)
    served_rows = incoming.reshape(group_size, grp_count * col_count)
    query_rows = served_rows[:, : HQ * HD]
    key_new = served_rows[:, HQ * HD : turned]
    value_new = served_rows[:, turned:]
    served_len = lengths[served_ids]
    served_table = page_table[served_ids]
    most_pages = page_table.shape[1]
    page_counts = (served_len + PAGE - 1) // PAGE
    logical = jnp.arange(most_pages, dtype=jnp.int32)
    pool_pages = k_cache.shape[1] // PAGE
    local_page = served_table - seq_index * pool_pages
    usable = (
        (logical[None, :] < page_counts[:, None]) & (local_page >= 0) & (local_page < pool_pages)
    )
    pool_ids = jnp.arange(pool_pages, dtype=jnp.int32)
    matched = usable[:, :, None] & (local_page[:, :, None] == pool_ids[None, None, :])
    owner_ids = jnp.arange(group_size, dtype=jnp.int32)
    page_owner = jnp.max(jnp.where(matched, owner_ids[:, None, None], -1), axis=(0, 1))
    page_number = jnp.max(jnp.where(matched, logical[None, :, None], 0), axis=(0, 1))
    present = page_owner >= 0
    holder = jnp.maximum(page_owner, 0)
    page_query = query_rows[holder].reshape(pool_pages, KVH, group_q, HD)
    page_keys = k_cache[0].reshape(pool_pages, PAGE, KVH, HD)
    page_values = v_cache[0].reshape(pool_pages, PAGE, KVH, HD)
    scores = (
        jnp.einsum("pkgd,ptkd->pkgt", page_query, page_keys, preferred_element_type=jnp.float32)
        * score_scale
    )
    places_in = page_number[:, None] * PAGE + jnp.arange(PAGE, dtype=jnp.int32)[None, :]
    alive_rows = present[:, None] & (places_in < served_len[holder][:, None])
    alive_wide = alive_rows[:, None, None, :]
    page_max = jnp.max(jnp.where(alive_wide, scores, neg_fill), axis=3)
    weights = jnp.exp(jnp.where(alive_wide, scores - page_max[..., None], neg_fill))
    page_total = jnp.sum(weights, axis=3).reshape(pool_pages, HQ)
    page_out = jnp.einsum(
        "pkgt,ptkd->pkgd",
        weights.astype(jnp.bfloat16),
        page_values,
        preferred_element_type=jnp.float32,
    ).reshape(pool_pages, HQ, HD)
    page_max = page_max.reshape(pool_pages, HQ)
    member = page_owner[:, None] == owner_ids[None, :]
    local_max = jnp.max(jnp.where(member[:, :, None], page_max[:, None, :], neg_fill), axis=0)
    factor = jnp.where(present[:, None], jnp.exp(page_max - local_max[holder]), 0.0)
    member_float = member.astype(jnp.float32)
    local_total = jnp.einsum(
        "pr,ph->rh", member_float, page_total * factor, precision=lax.Precision.HIGHEST
    )
    local_out = jnp.einsum(
        "pr,pe->re",
        member_float,
        (page_out * factor[..., None]).reshape(pool_pages, HQ * HD),
        precision=lax.Precision.HIGHEST,
    )
    new_score = (
        jnp.einsum(
            "rkgd,rkd->rkg",
            query_rows.reshape(group_size, KVH, group_q, HD),
            key_new.reshape(group_size, KVH, HD),
            preferred_element_type=jnp.float32,
        ).reshape(group_size, HQ)
        * score_scale
    )
    head_share = HQ // seq_count
    head_start = seq_index * head_share
    value_heads = jnp.broadcast_to(
        value_new.reshape(group_size, KVH, 1, HD), (group_size, KVH, group_q, HD)
    ).reshape(group_size, HQ, HD)
    value_here = lax.dynamic_slice_in_dim(value_heads, head_start, head_share, 1).astype(
        jnp.float32
    )
    new_here = lax.dynamic_slice_in_dim(new_score, head_start, head_share, 1)
    peak_score = lax.pmax(jnp.maximum(local_max, new_score), "seq")
    kept_scale = jnp.exp(local_max - peak_score)
    scaled_out = (local_out.reshape(group_size, HQ, HD) * kept_scale[..., None]).reshape(
        group_size, HQ * HD
    )
    shared_out, shared_total = (
        lax.psum_scatter(scaled_out, "seq", scatter_dimension=1, tiled=True),
        lax.psum_scatter(local_total * kept_scale, "seq", scatter_dimension=1, tiled=True),
    )
    peak_here = lax.dynamic_slice_in_dim(peak_score, head_start, head_share, 1)
    fresh_weight = jnp.exp(new_here - peak_here)
    denominator = shared_total + fresh_weight
    numerator = (
        shared_out.reshape(group_size, head_share, HD) + fresh_weight[..., None] * value_here
    )
    attended = (
        (numerator / denominator[..., None])
        .reshape(group_size, head_share * HD)
        .astype(jnp.bfloat16)
    )
    gathered = lax.all_gather(attended, "grp", axis=0, tiled=True)
    by_request = gathered[restore]
    return lax.psum_scatter(
        jnp.dot(by_request, w_out, preferred_element_type=jnp.float32).astype(jnp.bfloat16),
        "seq",
        scatter_dimension=0,
        tiled=True,
    )


def solution(mesh):
    placed = (
        P("grp", "seq"),
        P("seq", "grp"),
        P("grp"),
        P("seq", "grp"),
        P("grp", "seq", None),
        P("grp", "seq", None),
        P(),
        P(),
        P(),
        P(),
    )
    return jax.shard_map(
        shards, mesh=mesh, in_specs=placed, out_specs=P("seq", "grp"), check_vma=False
    )
```

profile of v0, /device:TPU:0, one launch (start us, length us, event | category | flops | bytes accessed | tf_op | source)
XLA Modules:
  0.0 401.5 jit_solution(12910051012480212838)
XLA Ops:
  6.5 9.0 %all_gather.6 = bf16[256,1024]{1,0:T(8,128)(2,1)S(1)} all-gather(bf16[64,1024]{1,0:T(8,128)(2,1)} %param.10), channel_id=1, replica_groups=mesh['seq'=8,'grp'=4] {'grp'}, dimensions={0}, use_global_device_ids=true | all-gather | bytes 655360 | tf_op jit(solution)/shard_map/all_gather | solution.py:57
  15.5 5.5 %fusion.40 = f32[256,2560]{1,0:T(8,128)} fusion(bf16[256,1024]{1,0:T(8,128)(2,1)S(1)} %all_gather.6, bf16[1024,2560]{1,0:T(8,128)(2,1)} %param.11), kind=kOutput, calls=%fused_computation.102 | convolution fusion | flops 1342177280 | bytes 8388608 | tf_op jit(solution)/shard_map/dot_general | solution.py:56
  24.9 113.1 %all-reduce.3.cloned.1.call-done = f32[256,2560]{1,0:T(8,128)} async-done(((f32[256,2560]{1,0:T(8,128)}), f32[256,2560]{1,0:T(8,128)}) %all-reduce.3.cloned.1.call-update) | async-done | bytes 2621456 | tf_op jit(solution)/shard_map/psum | solution.py:67
  138.0 3.6 broadcast_add_fusion
  141.6 2.1 copy.46
  144.1 2.1 copy.47
  146.2 11.8 %select_convert_fusion = bf16[256,2560]{1,0:T(8,128)(2,1)S(1)} fusion(f32[256,2560]{1,0:T(8,128)} %copy.47, f32[2560]{0:T(1024)S(1)} %multiply_exponential_fusion, f32[256]{0:T(256)S(1)} %bitcast.123, f32[256]{0:T(256)S(1)} %bitcast.124, f32[256]{0:T(256)S(1)} %bitcast.122, pred[2560]{0:T(1024)(128)(4,1)S(1)} %get-tuple-element.26, ...), kind=kLoop, calls=%fused_computation.12 | loop fusion | flops 5898240 | bytes 6584832 | tf_op jit(solution)/shard_map/convert_element_type | solution.py:68
  158.0 2.5 gather_fusion.3
  160.5 3.5 all-to-all-start
  165.1 8.8 %copy.68 = bf16[512,8,8,128]{3,2,1,0:T(8,128)(2,1)} copy(bf16[512,8,8,128]{3,1,2,0:T(8,128)(2,1)} %bitcast.100) | data formatting | bytes 16777216
  173.8 8.8 %copy.69 = bf16[512,8,8,128]{3,2,1,0:T(8,128)(2,1)} copy(bf16[512,8,8,128]{3,1,2,0:T(8,128)(2,1)} %bitcast.101) | data formatting | bytes 16777216
  184.9 1.7 gather_fusion.4
  187.8 6.9 %select_reduce_fusion.1 = (f32[32,8,8]{2,1,0:T(8,128)S(1)}, f32[32,8,8,128]{3,2,1,0:T(8,128)S(1)}) fusion(pred[32,128]{1,0:T(8,128)(4,1)S(1)} %fusion.25, bf16[32,8,8,128]{3,2,1,0:T(8,128)(2,1)S(1)} %bitcast.109, bf16[32,128,8,128]{3,2,1,0:T(8,128)(2,1)} %bitcast.97), kind=kOutput, calls=%fused_computation.26 | convolution fusion | flops 67893248 | bytes 9973760 | tf_op jit(solution)/shard_map/pkgd,ptkd->pkgt/dot_general | solution.py:98
  196.3 1.6 select_reduce_fusion
  197.9 2.0 gather_fusion.5
  205.6 35.0 %pmax.7 = f32[64,64]{0,1:T(8,128)S(1)} all-reduce(f32[64,64]{0,1:T(8,128)S(1)} %fusion.38), channel_id=1, replica_groups=mesh['seq'=8,'grp'=4] {'seq'}, use_global_device_ids=true, to_apply=%region_7.8 | all-reduce | flops 4096 | bytes 32768 | tf_op jit(solution)/shard_map/pmax | solution.py:145
  240.7 6.1 %fusion = f32[32,8,8,128]{3,2,1,0:T(8,128)S(1)} fusion(bf16[32,128,8,128]{3,2,1,0:T(8,128)(2,1)} %bitcast.96, f32[32,8,8,128]{3,2,1,0:T(8,128)S(1)} %get-tuple-element.21, f32[32,8,8]{2,1,0:T(8,128)S(1)} %get-tuple-element.20, pred[32,128]{1,0:T(8,128)(4,1)S(1)} %copy-done.6), kind=kOutput, calls=%fused_computation.7 | convolution fusion | flops 67895296 | bytes 10498048 | tf_op jit(solution)/shard_map/pkgt,ptkd->pkgd/dot_general | solution.py:107
  247.1 2.5 multiply_bitcast_fusion
  249.6 1.5 copy.96
  253.6 33.8 %all-reduce = f32[64,64]{0,1:T(8,128)S(1)} all-reduce(f32[64,64]{0,1:T(8,128)S(1)} %convolution_multiply_fusion), channel_id=3, replica_groups=mesh['seq'=8,'grp'=4] {'seq'}, use_global_device_ids=true, to_apply=%region_10.11.clone | all-reduce | flops 4096 | bytes 32768
  287.9 29.7 %reduce-scatter.3.cloned.1.call-done = f32[64,1024]{1,0:T(8,128)} async-done(((f32[64,8192]{1,0:T(8,128)}), f32[64,1024]{1,0:T(8,128)}) %reduce-scatter.3.cloned.1.call-update) | async-done | bytes 262160 | tf_op jit(solution)/shard_map/reduce_scatter | solution.py:151
  318.9 7.2 %all_gather.7 = bf16[256,1024]{1,0:T(8,128)(2,1)S(1)} all-gather(bf16[64,1024]{1,0:T(8,128)(2,1)S(1)} %bitcast.113), channel_id=1, replica_groups=mesh['seq'=8,'grp'=4] {'grp'}, dimensions={0}, use_global_device_ids=true | all-gather | bytes 655360 | tf_op jit(solution)/shard_map/all_gather | solution.py:165
  327.2 4.4 %convolution_convert_fusion = bf16[256,2048]{1,0:T(8,128)(2,1)} fusion(bf16[256,1024]{1,0:T(8,128)(2,1)S(1)} %gather_fusion.6, bf16[1024,2048]{1,0:T(8,128)(2,1)} %param.13), kind=kOutput, calls=%fused_computation.13 | convolution fusion | flops 1074266112 | bytes 5767168 | tf_op jit(solution)/shard_map/dot_general | solution.py:168
  331.7 63.3 %reduce-scatter.5.cloned.1.call-done = bf16[32,2048]{1,0:T(8,128)(2,1)} async-done(((bf16[256,2048]{1,0:T(8,128)(2,1)}), bf16[32,2048]{1,0:T(8,128)(2,1)}) %reduce-scatter.5.cloned.1.call-update) | async-done | bytes 131088 | tf_op jit(solution)/shard_map/reduce_scatter | solution.py:167
  (97 shorter events, 20.8 us)
Async XLA Ops:
  6.5 16.4 %copy-start = (s32[256,128]{1,0:T(8,128)S(1)}, s32[256,128]{1,0:T(8,128)}, u32[]{:S(2)}) copy-start(s32[256,128]{1,0:T(8,128)} %param.17) | copy-start | bytes 393220
  6.5 131.5 %all-reduce.3.cloned.1.call-start = ((), (), s32[]{:S(2)}) async-start(), calls=%async_computation.3 | async-start | bytes 5242880 | tf_op jit(solution)/shard_map/psum | solution.py:67
  21.0 0.7 copy-start.12
  21.0 1.1 copy-start.2
  21.0 2.5 copy-start.13
  21.0 117.0 %copy-start.8 = (f32[2560]{0:T(1024)S(1)}, f32[2560]{0:T(1024)}, u32[]{:S(2)}) copy-start(f32[2560]{0:T(1024)} %param.12) | copy-start | bytes 30724
  24.9 157.7 %copy-start.9 = (s32[32]{0:T(128)}, s32[32]{0:T(128)S(1)}, u32[]{:S(2)}) copy-start(s32[32]{0:T(128)S(1)} %get-tuple-element.6) | copy-start | bytes 388
  160.5 22.8 %all-to-all-start = ((bf16[4,64,2560]{2,1,0:T(8,128)(2,1)}), bf16[4,64,2560]{2,1,0:T(8,128)(2,1)S(1)}, u32[]{:S(2)}, u32[]{:S(2)}) async-start(bf16[4,64,2560]{2,1,0:T(8,128)(2,1)} %bitcast.8), calls=%async_computation | async-start | bytes 2621440 | tf_op jit(solution)/shard_map/all_to_all | solution.py:72
  164.1 153.6 %reduce-scatter.3.cloned.1.call-start = ((), (), s32[]{:S(2)}) async-start(), calls=%async_computation.4 | async-start | bytes 2359296 | tf_op jit(solution)/shard_map/reduce_scatter | solution.py:151
  164.3 20.6 %copy-start.11 = (s32[1024]{0:T(1024)}, s32[1024]{0:T(1024)S(1)}, u32[]{:S(2)}) copy-start(s32[1024]{0:T(1024)S(1)} %pad_clamp_fusion.2) | copy-start | bytes 12292
  182.6 2.0 copy-start.15
  183.4 4.4 %copy-start.5 = (pred[32,128]{1,0:T(8,128)(4,1)}, pred[32,128]{1,0:T(8,128)(4,1)S(1)}, u32[]{:S(2)}) copy-start(pred[32,128]{1,0:T(8,128)(4,1)S(1)} %fusion.25) | copy-start | bytes 12292
  202.1 3.5 copy-start.4
  203.5 37.2 %copy-start.6 = (pred[32,128]{1,0:T(8,128)(4,1)S(1)}, pred[32,128]{1,0:T(8,128)(4,1)}, u32[]{:S(2)}) copy-start(pred[32,128]{1,0:T(8,128)(4,1)} %copy-done.5) | copy-start | bytes 12292
  240.7 6.1 %copy-start.7 = (f32[32,64]{1,0:T(8,128)S(1)}, f32[32,64]{1,0:T(8,128)}, u32[]{:S(2)}) copy-start(f32[32,64]{1,0:T(8,128)} %exponential_select_fusion) | copy-start | bytes 24580
  240.7 6.4 %copy-start.10 = (s32[32]{0:T(128)S(1)}, s32[32]{0:T(128)}, u32[]{:S(2)}) copy-start(s32[32]{0:T(128)} %copy-done.9) | copy-start | bytes 388
  249.6 1.6 copy-start.16
  249.6 2.9 copy-start.14
  251.1 36.5 %copy-start.3 = (bf16[8,8,8,128]{3,1,2,0:T(8,128)(2,1)S(1)}, bf16[8,8,8,128]{3,1,2,0:T(8,128)(2,1)}, u32[]{:S(2)}) copy-start(bf16[8,8,8,128]{3,1,2,0:T(8,128)(2,1)} %get-tuple-element.13) | copy-start | bytes 393220
  251.1 143.9 %reduce-scatter.5.cloned.1.call-start = ((), (), s32[]{:S(2)}) async-start(), calls=%async_computation.5 | async-start | bytes 1179648 | tf_op jit(solution)/shard_map/reduce_scatter | solution.py:167
  326.1 68.9 %copy-start.1 = (s32[256,128]{1,0:T(8,128)S(1)}, s32[256,128]{1,0:T(8,128)}, u32[]{:S(2)}) copy-start(s32[256,128]{1,0:T(8,128)} %param.17) | copy-start | bytes 393220
Sparse Core Ops, SparseCore 0:
  21.2 116.7 all-reduce.2
  251.2 66.3 reduce-scatter.2
  331.8 63.1 reduce-scatter.4
where the time goes:
time: 402 us
  waiting for transfers between devices  206 us (51%)
  blocking collectives  84.9 us (21%)
  local copies, waits for them, and re-layouts  43.9 us (11%)
  matrix products  26.3 us (7%)
  other arithmetic  22.2 us (6%)
  between operations  14.2 us (4%)
    psum x1, waiting for transfers between devices, shards(): summed = lax.psum(partial_sum, 'seq')  113 us
    reduce_scatter x1, waiting for transfers between devices, shards(): lax.psum_scatter(jnp.dot(by_request, w_out, preferred_element_type=jnp.fl...  63.3 us
    pmax x1, blocking collectives, shards(): peak_score = lax.pmax(jnp.maximum(local_max, new_score), 'seq')  35 us
    unnamed x1, blocking collectives  33.8 us
    reduce_scatter x1, waiting for transfers between devices, shards(): lax.psum_scatter(scaled_out, 'seq', scatter_dimension=1, tiled=True)  29.7 us
    unnamed x45, local copies, waits for them, and re-layouts  22.6 us
    convert_element_type x1, other arithmetic, shards(): rotate_heads(summed + b_qkv[None, :], positions, col_start, HD, turned)  11.8 us
    all_gather x1, blocking collectives, shards(): lax.all_gather(hidden, 'grp', axis=0, tiled=True)  8.97 us
  transfers between devices with their start and end apart: 4, of which 3 were waited for; matrix products, arithmetic and copies ran while one was open for 6% of the time, Pallas kernels for 0%

commit v1 on v0

v1 whole, which is shorter than its diff:
```python
import functools
import math

import jax
import jax.numpy as jnp
from jax import lax
from jax.experimental import pallas as pl
from jax.experimental.pallas import tpu as pltpu
from jax.sharding import PartitionSpec as P

HQ = 64
KVH = 8
HD = 128
PAGE = 128


rope_base = 1000000.0
neg_fill = -1e30


def rotate_heads(values, places, col_start, head_dim, turned):
    row_count, col_count = values.shape
    columns = col_start + jnp.arange(col_count, dtype=jnp.int32)
    within = columns % head_dim
    freq_index = within % (head_dim // 2)
    inverse_freq = jnp.exp(freq_index.astype(jnp.float32) * (-2.0 * math.log(rope_base) / head_dim))
    section = jnp.where(
        freq_index < head_dim // 8,
        0,
        jnp.where(freq_index < head_dim // 8 + 3 * head_dim // 16, 1, 2),
    )
    place_float = places.astype(jnp.float32)
    chosen = jnp.where(
        section[None, :] == 0,
        place_float[0][:, None],
        jnp.where(section[None, :] == 1, place_float[1][:, None], place_float[2][:, None]),
    )
    angles = chosen * inverse_freq[None, :]
    halves = values.reshape(row_count, col_count // head_dim, 2, head_dim // 2)
    partner = jnp.concatenate([-halves[:, :, 1:], halves[:, :, :1]], axis=2).reshape(
        row_count, col_count
    )
    rotated = values * jnp.cos(angles) + partner * jnp.sin(angles)
    return jnp.where((columns < turned)[None, :], rotated, values)


def attend_pages(block_pages, owner_ref, live_ref, rows_ref, key_ref, value_ref, out_ref, stat_ref):
    step = pl.program_id(0)
    group_q = HQ // KVH
    width = KVH * HD

    @pl.when(step == 0)
    def _():
        out_ref[...] = jnp.zeros_like(out_ref)
        lanes = lax.broadcasted_iota(jnp.int32, stat_ref.shape, 2)
        stat_ref[...] = jnp.where(lanes < HD // 2, neg_fill, 0.0)

    row_head = lax.broadcasted_iota(jnp.int32, (HQ, width), 0) // group_q
    col_head = lax.broadcasted_iota(jnp.int32, (HQ, width), 1) // HD
    own_head = (row_head == col_head).astype(jnp.float32).astype(jnp.bfloat16)
    place = lax.broadcasted_iota(jnp.int32, (HQ, PAGE), 1)
    lane = lax.broadcasted_iota(jnp.int32, (HQ, HD), 1)
    pages = []
    for j in range(block_pages):
        owner = owner_ref[step * block_pages + j]
        alive = place < live_ref[step * block_pages + j]
        query = rows_ref[owner, :HQ, :]
        spread = jnp.concatenate([query] * KVH, axis=1) * own_head
        keys = key_ref[0, j * PAGE : (j + 1) * PAGE, :]
        values = value_ref[0, j * PAGE : (j + 1) * PAGE, :]
        scores = lax.dot_general(
            spread, keys, (((1,), (1,)), ((), ())), preferred_element_type=jnp.float32
        ) * (HD**-0.5)
        scores = jnp.where(alive, scores, neg_fill)
        page_max = jnp.max(scores, axis=1, keepdims=True)
        weights = jnp.where(alive, jnp.exp(scores - page_max), 0.0)
        page_total = jnp.sum(weights, axis=1, keepdims=True)
        wide = jnp.dot(weights.astype(jnp.bfloat16), values, preferred_element_type=jnp.float32)
        page_out = jnp.concatenate(
            [
                wide[h * group_q : (h + 1) * group_q, h * HD : (h + 1) * HD]
                for h in range(KVH)
            ],
            axis=0,
        )
        pages.append((owner, page_max, page_total, page_out))
    for owner, page_max, page_total, page_out in pages:
        stat = stat_ref[owner]
        old_max = stat[:, :1]
        new_max = jnp.maximum(old_max, page_max)
        kept = jnp.exp(old_max - new_max)
        added = jnp.exp(page_max - new_max)
        out_ref[owner] = out_ref[owner] * kept + page_out * added
        total = stat[:, HD // 2 : HD // 2 + 1] * kept + page_total * added
        stat_ref[owner] = jnp.where(lane < HD // 2, new_max, total)


def local_attention(owner, live, rows, k_cache, v_cache):
    group_size = rows.shape[0]
    pool_pages = k_cache.shape[1] // PAGE
    block_pages = math.gcd(pool_pages, 4)
    cache_spec = pl.BlockSpec((1, block_pages * PAGE, KVH * HD), lambda i, *_: (0, i, 0))
    whole_spec = pl.BlockSpec((group_size, HQ, HD), lambda i, *_: (0, 0, 0))
    shape = jax.ShapeDtypeStruct((group_size, HQ, HD), jnp.float32)
    return pl.pallas_call(
        functools.partial(attend_pages, block_pages),
        grid_spec=pltpu.PrefetchScalarGridSpec(
            num_scalar_prefetch=2,
            grid=(pool_pages // block_pages,),
            in_specs=[
                pl.BlockSpec(rows.shape, lambda i, *_: (0, 0, 0)),
                cache_spec,
                cache_spec,
            ],
            out_specs=[whole_spec, whole_spec],
        ),
        out_shape=[shape, shape],
        compiler_params=pltpu.CompilerParams(
            dimension_semantics=("arbitrary",), vmem_limit_bytes=40 * 1024 * 1024
        ),
        cost_estimate=pl.CostEstimate(
            flops=4 * pool_pages * HQ * PAGE * KVH * HD,
            bytes_accessed=4 * pool_pages * PAGE * KVH * HD,
            transcendentals=pool_pages * HQ * PAGE,
        ),
    )(owner, live, rows, k_cache, v_cache)


def shards(hidden, w_qkv, b_qkv, w_out, k_cache, v_cache, lengths, page_table, positions, group_of):
    seq_count = lax.axis_size("seq")
    grp_count = lax.axis_size("grp")
    seq_index = lax.axis_index("seq")
    grp_index = lax.axis_index("grp")
    request_total = group_of.shape[0]
    group_size = request_total // grp_count
    share = group_size // seq_count
    col_count = w_qkv.shape[1]
    col_start = grp_index * col_count
    turned = (HQ + KVH) * HD
    group_q = HQ // KVH
    score_scale = HD ** (-0.5)
    request_ids = jnp.arange(request_total, dtype=jnp.int32)
    before = (group_of[None, :] < group_of[:, None]) | (group_of[None, :] == group_of[:, None]) & (
        request_ids[None, :] < request_ids[:, None]
    )
    restore = jnp.sum(before.astype(jnp.int32), axis=1)
    placed_at = restore[None, :] == request_ids[:, None]
    served_order = jnp.sum(jnp.where(placed_at, request_ids[None, :], 0), axis=1)
    served_ids = lax.dynamic_slice_in_dim(served_order, grp_index * group_size, group_size, 0)
    send_order = (
        served_order.reshape(grp_count, seq_count, share).transpose(1, 0, 2).reshape(request_total)
    )
    hidden_all = lax.all_gather(hidden, "grp", axis=0, tiled=True)[send_order]
    partial_sum = jnp.dot(hidden_all, w_qkv, preferred_element_type=jnp.float32)
    summed = lax.psum_scatter(partial_sum, "seq", scatter_dimension=0, tiled=True)
    row_share = request_total // seq_count
    my_rows = lax.dynamic_slice_in_dim(send_order, seq_index * row_share, row_share, 0)
    fresh_rows = rotate_heads(
        summed + b_qkv[None, :], positions[:, my_rows], col_start, HD, turned
    ).astype(jnp.bfloat16)
    outgoing = fresh_rows.reshape(grp_count, share, col_count)
    incoming = lax.all_to_all(outgoing, "grp", split_axis=0, concat_axis=2, tiled=True)
    head_rows = incoming.reshape(share, grp_count * col_count // HD, HD)
    rows = lax.all_gather(head_rows, "seq", axis=0, tiled=True)

    served_len = lengths[served_ids]
    served_table = page_table[served_ids]
    most_pages = page_table.shape[1]
    page_counts = (served_len + PAGE - 1) // PAGE
    logical = jnp.arange(most_pages, dtype=jnp.int32)
    pool_pages = k_cache.shape[1] // PAGE
    local_page = served_table - seq_index * pool_pages
    usable = (
        (logical[None, :] < page_counts[:, None]) & (local_page >= 0) & (local_page < pool_pages)
    )
    pool_ids = jnp.arange(pool_pages, dtype=jnp.int32)
    matched = usable[:, :, None] & (local_page[:, :, None] == pool_ids[None, None, :])
    owner_ids = jnp.arange(group_size, dtype=jnp.int32)
    left = served_len[:, None] - logical[None, :] * PAGE
    live = jnp.max(jnp.where(matched, left[:, :, None], 0), axis=(0, 1))
    owner = jnp.max(jnp.where(matched, owner_ids[:, None, None], 0), axis=(0, 1))
    local_out, local_stat = local_attention(owner, live, rows, k_cache, v_cache)

    head_share = HQ // seq_count
    head_start = seq_index * head_share
    kv_share = max(1, head_share // group_q)
    kv_start = head_start // group_q
    query_here = lax.dynamic_slice_in_dim(rows, head_start, head_share, 1).astype(jnp.float32)
    key_here = lax.dynamic_slice_in_dim(rows, HQ + kv_start, kv_share, 1).astype(jnp.float32)
    value_here = lax.dynamic_slice_in_dim(rows, HQ + KVH + kv_start, kv_share, 1).astype(
        jnp.float32
    )
    key_here = jnp.repeat(key_here, head_share // kv_share, axis=1)
    value_here = jnp.repeat(value_here, head_share // kv_share, axis=1)
    new_here = jnp.sum(query_here * key_here, axis=2) * score_scale

    out_parts = lax.all_to_all(
        local_out.astype(jnp.bfloat16)
        .reshape(group_size, seq_count, head_share * HD)
        .transpose(1, 0, 2),
        "seq",
        split_axis=0,
        concat_axis=0,
        tiled=True,
    )
    stats = jnp.stack([local_stat[:, :, 0], local_stat[:, :, HD // 2]], axis=0)
    stats = stats.reshape(2, group_size, seq_count, head_share).transpose(2, 0, 1, 3)
    stat_parts = lax.all_to_all(
        stats.reshape(seq_count, 2 * group_size * head_share),
        "seq",
        split_axis=0,
        concat_axis=0,
        tiled=True,
    ).reshape(seq_count, 2, group_size, head_share)
    part_max = stat_parts[:, 0]
    part_total = stat_parts[:, 1]
    peak_here = jnp.maximum(jnp.max(part_max, axis=0), new_here)
    factor = jnp.exp(part_max - peak_here[None])
    fresh_weight = jnp.exp(new_here - peak_here)
    denominator = jnp.sum(part_total * factor, axis=0) + fresh_weight

    def widen(small):
        return jnp.repeat(small, HD, axis=-1)

    numerator = jnp.sum(out_parts.astype(jnp.float32) * widen(factor), axis=0) + widen(
        fresh_weight
    ) * value_here.reshape(group_size, head_share * HD)
    attended = (numerator / widen(denominator)).astype(jnp.bfloat16)
    gathered = lax.all_gather(attended, "grp", axis=0, tiled=True)
    by_request = gathered[restore]
    mixed = jnp.dot(by_request, w_out, preferred_element_type=jnp.float32).astype(jnp.bfloat16)
    mixed_parts = lax.all_to_all(
        mixed.reshape(seq_count, row_share, mixed.shape[1]),
        "seq",
        split_axis=0,
        concat_axis=0,
        tiled=True,
    )
    return jnp.sum(mixed_parts.astype(jnp.float32), axis=0).astype(jnp.bfloat16)


def solution(mesh):
    placed = (
        P("grp", "seq"),
        P("seq", "grp"),
        P("grp"),
        P("seq", "grp"),
        P("grp", "seq", None),
        P("grp", "seq", None),
        P(),
        P(),
        P(),
        P(),
    )
    return jax.shard_map(
        shards, mesh=mesh, in_specs=placed, out_specs=P("seq", "grp"), check_vma=False
    )
```

time: 402 us -> 269 us (0.67)
  waiting for transfers between devices: 206 us -> 128 us
  blocking collectives: 84.9 us -> 53 us
  Pallas kernels: 0 us -> 18.3 us
  matrix products: 26.3 us -> 8.95 us
  local copies, waits for them, and re-layouts: 43.9 us -> 27.8 us
  other arithmetic: 22.2 us -> 11.6 us
    psum x1 -> x0, waiting for transfers between devices: 113 us -> none  [shards(): summed = lax.psum(partial_sum, 'seq')]
    all_gather x0 -> x1, waiting for transfers between devices: none -> 37.9 us  [shards(): rows = lax.all_gather(head_rows, 'seq', axis=0, tiled=True)]
    all_to_all x0 -> x2, blocking collectives: none -> 37 us  [the longest x1 29.5 us: shards(): lax.all_to_all(mixed.reshape(seq_count, row_share, mixed.shape[1]), 'seq'...]
    pmax x1 -> x0, blocking collectives: 35 us -> none  [shards(): peak_score = lax.pmax(jnp.maximum(local_max, new_score), 'seq')]
    unnamed x1 -> x0, blocking collectives: 33.8 us -> none
    reduce_scatter x2 -> x1, waiting for transfers between devices: 93.1 us -> 70.3 us  [shards(): lax.psum_scatter(partial_sum, 'seq', scatter_dimension=0, tiled=True)]
    all_to_all x1 -> x2, waiting for transfers between devices: 0.01 us -> 19.7 us  [the longest x1 15.4 us: shards(): lax.all_to_all(local_out.astype(jnp.bfloat16).reshape(group_size, seq_cou...]
    pallas_call x0 -> x1, Pallas kernels: none -> 18.3 us  [local_attention(): pl.pallas_call(functools.partial(attend_pages, block_pages), grid_spec=pl...]
  transfers between devices with their start and end apart: 4 -> 4, of which waited for: 3 -> 4; matrix products, arithmetic and copies ran while one was open for 6% -> 5% of each run, Pallas kernels for 0% -> 0%
where the time goes in v1:
time: 269 us; the launch traced here: 268 us
  waiting for transfers between devices  128 us (48%)
  blocking collectives  53 us (20%)
  local copies, waits for them, and re-layouts  27.8 us (10%)
  Pallas kernels  18.3 us (7%)
  between operations  13.7 us (5%)
  other arithmetic  11.6 us (4%)
  matrix products  8.95 us (3%)
  starting transfers between devices  7.12 us (3%)
    reduce_scatter x1, waiting for transfers between devices, shards(): lax.psum_scatter(partial_sum, 'seq', scatter_dimension=0, tiled=True)  70.3 us
    all_gather x1, waiting for transfers between devices, shards(): rows = lax.all_gather(head_rows, 'seq', axis=0, tiled=True)  37.9 us
    all_to_all x1, blocking collectives, shards(): lax.all_to_all(mixed.reshape(seq_count, row_share, mixed.shape[1]), 'seq'...  29.5 us
    pallas_call x1, Pallas kernels, local_attention(): pl.pallas_call(functools.partial(attend_pages, block_pages), grid_spec=pl...  18.3 us
    all_to_all x1, waiting for transfers between devices, shards(): lax.all_to_all(local_out.astype(jnp.bfloat16).reshape(group_size, seq_cou...  15.4 us
    all_gather x1, blocking collectives, shards(): hidden_all = lax.all_gather(hidden, 'grp', axis=0, tiled=True)[send_order]  8.86 us
    slice x3, local copies, waits for them, and re-layouts, shards(): stats = jnp.stack([local_stat[:, :, 0], local_stat[:, :, HD // 2]], axis=0)  8.08 us
    all_to_all x1, blocking collectives, shards(): lax.all_to_all(outgoing, 'grp', split_axis=0, concat_axis=2, tiled=True)  7.52 us
  transfers between devices with their start and end apart: 4, of which 4 were waited for; matrix products, arithmetic and copies ran while one was open for 5% of the time, Pallas kernels for 0%

profile of v1, /device:TPU:0, one launch (start us, length us, event | category | flops | bytes accessed | tf_op | source)
XLA Modules:
  0.0 268.4 jit_solution(10936518002452286061)
XLA Ops:
  7.8 8.9 %all_gather.9 = bf16[256,1024]{1,0:T(8,128)(2,1)S(1)} all-gather(bf16[64,1024]{1,0:T(8,128)(2,1)} %param.10), channel_id=1, replica_groups=mesh['seq'=8,'grp'=4] {'grp'}, dimensions={0}, use_global_device_ids=true | all-gather | bytes 655360 | tf_op jit(solution)/shard_map/all_gather | solution.py:153
  16.7 1.2 gather_fusion.2
  17.9 5.5 %fusion.21 = f32[256,2560]{1,0:T(8,128)} fusion(bf16[256,1024]{1,0:T(8,128)(2,1)S(1)} %gather_fusion.2, bf16[1024,2560]{1,0:T(8,128)(2,1)} %param.11), kind=kOutput, calls=%fused_computation.82 | convolution fusion | flops 1342177280 | bytes 8388608 | tf_op jit(solution)/shard_map/dot_general | solution.py:154
  25.1 70.3 %reduce-scatter.2.cloned.1.call-done = f32[32,2560]{1,0:T(8,128)} async-done(((f32[256,2560]{1,0:T(8,128)}), f32[32,2560]{1,0:T(8,128)}) %reduce-scatter.2.cloned.1.call-update) | async-done | bytes 327696 | tf_op jit(solution)/shard_map/reduce_scatter | solution.py:155
  98.7 1.4 fusion.7
  100.2 7.5 %all_to_all.35 = bf16[4,8,2560]{2,1,0:T(8,128)(2,1)S(1)} all-to-all(bf16[4,8,2560]{2,1,0:T(8,128)(2,1)S(1)} %fusion.7), channel_id=1, replica_groups=mesh['seq'=8,'grp'=4] {'grp'}, dimensions={0} | all-to-all | bytes 327680 | tf_op jit(solution)/shard_map/all_to_all | solution.py:162
  110.8 37.9 %all-gather.2.cloned.1.call-done.rows_ref = bf16[64,80,128]{2,1,0:T(8,128)(2,1)} async-done(((bf16[8,80,128]{2,1,0:T(8,128)(2,1)}), bf16[64,80,128]{2,1,0:T(8,128)(2,1)}) %all-gather.2.cloned.1.call-update) | async-done | bytes 1310736 | tf_op jit(solution)/shard_map/all_gather | solution.py:164
  148.7 3.4 %copy-done.1 = bf16[1,4096,1024]{2,1,0:T(8,128)(2,1)S(1)} copy-done((bf16[1,4096,1024]{2,1,0:T(8,128)(2,1)S(1)}, bf16[1,4096,1024]{2,1,0:T(8,128)(2,1)}, u32[]{:S(2)}) %copy-start.1) | copy-done | bytes 8388632
  152.1 1.3 copy-done.2
  153.4 18.3 %shard_map.100 = (f32[64,64,128]{2,1,0:T(8,128)S(1)}, f32[64,64,128]{2,1,0:T(8,128)S(1)}) custom-call(s32[32]{0:T(128)S(1)} %get-tuple-element.10.owner_ref, s32[32]{0:T(128)S(1)} %get-tuple-element.9.live_ref, bf16[64,80,128]{2,1,0:T(8,128)(2,1)S(1)} %copy-done.2, bf16[1,4096,1024]{2,1,0:T(8,128)(2,1)S(1)} %copy-done.1, bf16[1,4096,1024]{2,1,0:T(8,128)(2,1)} %value_ref.1), custom_call_target="tpu_custom_call" | custom-call | flops 1073741824 | bytes 16777216 | tf_op jit(solution)/shard_map/pallas_call | solution.py:105
  171.7 2.8 %fusion.20 = (f32[64,64,1]{2,1,0:T(8,128)}, f32[64,64,1]{2,1,0:T(8,128)}) fusion(f32[64,64,128]{2,1,0:T(8,128)S(1)} %get-tuple-element.8), kind=kLoop, calls=%fused_computation.81 | loop fusion | bytes 65536 | tf_op jit(solution)/shard_map/slice | solution.py:206
  174.6 2.6 copy.53
  177.2 2.6 copy.54
  180.9 3.5 %all-to-all-start.2 = ((f32[8,1,1024]{2,1,0:T(1,128)}), f32[8,1,1024]{2,1,0:T(1,128)S(1)}, u32[]{:S(2)}, u32[]{:S(2)}) async-start(f32[8,1,1024]{2,1,0:T(1,128)} %all_to_all.30), calls=%async_computation.3 | async-start | bytes 65536 | tf_op jit(solution)/shard_map/all_to_all | solution.py:208
  185.2 1.6 copy.64
  186.7 4.3 %all-to-all-done.2 = f32[8,1,1024]{2,1,0:T(1,128)S(1)} async-done(((f32[8,1,1024]{2,1,0:T(1,128)}), f32[8,1,1024]{2,1,0:T(1,128)S(1)}, u32[]{:S(2)}, u32[]{:S(2)}) %all-to-all-start.2) | async-done | bytes 32800 | tf_op jit(solution)/shard_map/all_to_all | solution.py:208
  191.1 3.6 %all-to-all-start.1 = ((bf16[8,64,1024]{2,1,0:T(8,128)(2,1)}), bf16[8,64,1024]{2,1,0:T(8,128)(2,1)S(1)}, u32[]{:S(2)}, u32[]{:S(2)}) async-start(bf16[8,64,1024]{2,1,0:T(8,128)(2,1)} %bitcast.52), calls=%async_computation.2 | async-start | bytes 2097152 | tf_op jit(solution)/shard_map/all_to_all | solution.py:197
  194.7 1.6 dynamic-slice_convert_fusion
  197.9 2.0 broadcast_in_dim.159
  199.8 1.7 reshape.244
  203.1 15.4 %all-to-all-done.1 = bf16[8,64,1024]{2,1,0:T(8,128)(2,1)S(1)} async-done(((bf16[8,64,1024]{2,1,0:T(8,128)(2,1)}), bf16[8,64,1024]{2,1,0:T(8,128)(2,1)S(1)}, u32[]{:S(2)}, u32[]{:S(2)}) %all-to-all-start.1) | async-done | bytes 1048608 | tf_op jit(solution)/shard_map/all_to_all | solution.py:197
  219.5 7.1 %all_gather.11 = bf16[256,1024]{1,0:T(8,128)(2,1)S(1)} all-gather(bf16[64,1024]{1,0:T(8,128)(2,1)S(1)} %fusion.1), channel_id=1, replica_groups=mesh['seq'=8,'grp'=4] {'grp'}, dimensions={0}, use_global_device_ids=true | all-gather | bytes 655360 | tf_op jit(solution)/shard_map/all_gather | solution.py:229
  227.8 3.4 %convolution_convert_fusion = bf16[256,2048]{1,0:T(8,128)(2,1)S(1)} fusion(bf16[256,1024]{1,0:T(8,128)(2,1)S(1)} %gather_fusion.4, bf16[1024,2048]{1,0:T(8,128)(2,1)} %param.13), kind=kOutput, calls=%fused_computation.5 | convolution fusion | flops 1074266112 | bytes 5767168 | tf_op jit(solution)/shard_map/dot_general | solution.py:231
  231.2 29.5 %all_to_all.36 = bf16[8,32,2048]{2,1,0:T(8,128)(2,1)S(1)} all-to-all(bf16[8,32,2048]{2,1,0:T(8,128)(2,1)S(1)} %bitcast.55), channel_id=1, replica_groups=mesh['seq'=8,'grp'=4] {'seq'}, dimensions={0} | all-to-all | bytes 2097152 | tf_op jit(solution)/shard_map/all_to_all | solution.py:232
  (70 shorter events, 17.1 us)
Async XLA Ops:
  6.5 102.9 %copy-start = (s32[256,128]{1,0:T(8,128)S(1)}, s32[256,128]{1,0:T(8,128)}, u32[]{:S(2)}) copy-start(s32[256,128]{1,0:T(8,128)} %param.17) | copy-start | bytes 393220
  6.5 88.9 %reduce-scatter.2.cloned.1.call-start = ((), (), s32[]{:S(2)}) async-start(), calls=%async_computation.5 | async-start | bytes 2949120 | tf_op jit(solution)/shard_map/reduce_scatter | solution.py:155
  23.4 0.7 copy-start.7
  23.4 72.0 %copy-start.6 = (f32[2560]{0:T(1024)S(1)}, f32[2560]{0:T(1024)}, u32[]{:S(2)}) copy-start(f32[2560]{0:T(1024)} %param.12) | copy-start | bytes 30724
  23.4 125.3 %all-gather.2.cloned.1.call-start = ((), (), s32[]{:S(2)}) async-start(), calls=%async_computation.6 | async-start | bytes 1474560 | tf_op jit(solution)/shard_map/all_gather | solution.py:164
  96.4 2.3 copy-start.4
  97.4 11.2 %copy-start.3 = (s32[256]{0:T(256)S(1)}, s32[256]{0:T(256)}, u32[]{:S(2)}) copy-start(s32[256]{0:T(256)} %param.16) | copy-start | bytes 3076
  148.7 3.4 %copy-start.1 = (bf16[1,4096,1024]{2,1,0:T(8,128)(2,1)S(1)}, bf16[1,4096,1024]{2,1,0:T(8,128)(2,1)}, u32[]{:S(2)}) copy-start(bf16[1,4096,1024]{2,1,0:T(8,128)(2,1)} %key_ref.1) | copy-start | bytes 25165828
  152.1 1.3 copy-start.2
  180.9 10.1 %all-to-all-start.2 = ((f32[8,1,1024]{2,1,0:T(1,128)}), f32[8,1,1024]{2,1,0:T(1,128)S(1)}, u32[]{:S(2)}, u32[]{:S(2)}) async-start(f32[8,1,1024]{2,1,0:T(1,128)} %all_to_all.30), calls=%async_computation.3 | async-start | bytes 65536 | tf_op jit(solution)/shard_map/all_to_all | solution.py:208
  191.1 27.4 %all-to-all-start.1 = ((bf16[8,64,1024]{2,1,0:T(8,128)(2,1)}), bf16[8,64,1024]{2,1,0:T(8,128)(2,1)S(1)}, u32[]{:S(2)}, u32[]{:S(2)}) async-start(bf16[8,64,1024]{2,1,0:T(8,128)(2,1)} %bitcast.52), calls=%async_computation.2 | async-start | bytes 2097152 | tf_op jit(solution)/shard_map/all_to_all | solution.py:197
  218.5 0.8 copy-start.5
Sparse Core Ops, SparseCore 0:
  23.5 71.8 reduce-scatter.1
  108.7 39.9 all-gather.1

commit v2 on v1

--- a/solution.py
+++ b/solution.py
@@ -36,9 +36,9 @@
         jnp.where(section[None, :] == 1, place_float[1][:, None], place_float[2][:, None]),
     )
     angles = chosen * inverse_freq[None, :]
-    halves = values.reshape(row_count, col_count // head_dim, 2, head_dim // 2)
-    partner = jnp.concatenate([-halves[:, :, 1:], halves[:, :, :1]], axis=2).reshape(
-        row_count, col_count
+    half = head_dim // 2
+    partner = jnp.where(
+        (within < half)[None, :], -jnp.roll(values, -half, axis=1), jnp.roll(values, half, axis=1)
     )
     rotated = values * jnp.cos(angles) + partner * jnp.sin(angles)
     return jnp.where((columns < turned)[None, :], rotated, values)
@@ -116,7 +116,7 @@
         ),
         out_shape=[shape, shape],
         compiler_params=pltpu.CompilerParams(
-            dimension_semantics=("arbitrary",), vmem_limit_bytes=40 * 1024 * 1024
+            dimension_semantics=("arbitrary",), vmem_limit_bytes=58 * 1024 * 1024
         ),
         cost_estimate=pl.CostEstimate(
             flops=4 * pool_pages * HQ * PAGE * KVH * HD,
@@ -152,8 +152,17 @@
     )
     hidden_all = lax.all_gather(hidden, "grp", axis=0, tiled=True)[send_order]
     partial_sum = jnp.dot(hidden_all, w_qkv, preferred_element_type=jnp.float32)
-    summed = lax.psum_scatter(partial_sum, "seq", scatter_dimension=0, tiled=True)
     row_share = request_total // seq_count
+    summed = jnp.sum(
+        lax.all_to_all(
+            partial_sum.reshape(seq_count, row_share, col_count),
+            "seq",
+            split_axis=0,
+            concat_axis=0,
+            tiled=True,
+        ),
+        axis=0,
+    )
     my_rows = lax.dynamic_slice_in_dim(send_order, seq_index * row_share, row_share, 0)
     fresh_rows = rotate_heads(
         summed + b_qkv[None, :], positions[:, my_rows], col_start, HD, turned
@@ -161,7 +170,13 @@
     outgoing = fresh_rows.reshape(grp_count, share, col_count)
     incoming = lax.all_to_all(outgoing, "grp", split_axis=0, concat_axis=2, tiled=True)
     head_rows = incoming.reshape(share, grp_count * col_count // HD, HD)
-    rows = lax.all_gather(head_rows, "seq", axis=0, tiled=True)
+    rows = lax.all_to_all(
+        jnp.broadcast_to(head_rows[None], (seq_count,) + head_rows.shape),
+        "seq",
+        split_axis=0,
+        concat_axis=0,
+        tiled=True,
+    ).reshape((group_size,) + head_rows.shape[1:])
 
     served_len = lengths[served_ids]
     served_table = page_table[served_ids]

time: 269 us -> 242 us (0.90)
  waiting for transfers between devices: 128 us -> 107 us
  between operations: 13.7 us -> 0.33 us
  starting transfers between devices: 7.12 us -> 17 us
  local copies, waits for them, and re-layouts: 27.8 us -> 23.8 us
    all_to_all x0 -> x2, waiting for transfers between devices: none -> 87.4 us  [the longest x1 58.5 us: shards(): lax.all_to_all(partial_sum.reshape(seq_count, row_share, col_count), 'seq...]
    reduce_scatter x1 -> x0, waiting for transfers between devices: 70.3 us -> none  [shards(): lax.psum_scatter(partial_sum, 'seq', scatter_dimension=0, tiled=True)]
    all_gather x1 -> x0, waiting for transfers between devices: 37.9 us -> none  [shards(): rows = lax.all_gather(head_rows, 'seq', axis=0, tiled=True)]
    all_to_all x0 -> x2, starting transfers between devices: none -> 9.6 us  [the longest x1 5.97 us: shards(): lax.all_to_all(partial_sum.reshape(seq_count, row_share, col_count), 'seq...]
    unnamed x17 -> x13, local copies, waits for them, and re-layouts: 5.81 us -> 1.7 us
  transfers between devices with their start and end apart: 4 -> 4, of which waited for: 4 -> 4; matrix products, arithmetic and copies ran while one was open for 5% -> 7% of each run, Pallas kernels for 0% -> 0%
where the time goes in v2:
time: 242 us; the launch traced here: 241 us
  waiting for transfers between devices  107 us (44%)
  blocking collectives  52.5 us (22%)
  local copies, waits for them, and re-layouts  23.8 us (10%)
  Pallas kernels  20.5 us (8%)
  starting transfers between devices  17 us (7%)
  other arithmetic  11.7 us (5%)
  matrix products  8.95 us (4%)
    all_to_all x1, waiting for transfers between devices, shards(): lax.all_to_all(partial_sum.reshape(seq_count, row_share, col_count), 'seq...  58.5 us
    all_to_all x1, blocking collectives, shards(): lax.all_to_all(mixed.reshape(seq_count, row_share, mixed.shape[1]), 'seq'...  29.9 us
    all_to_all x1, waiting for transfers between devices, shards(): lax.all_to_all(jnp.broadcast_to(head_rows[None], (seq_count,) + head_rows...  28.8 us
    pallas_call x1, Pallas kernels, local_attention(): pl.pallas_call(functools.partial(attend_pages, block_pages), grid_spec=pl...  20.5 us
    all_to_all x1, waiting for transfers between devices, shards(): lax.all_to_all(local_out.astype(jnp.bfloat16).reshape(group_size, seq_cou...  16.6 us
    all_gather x1, blocking collectives, shards(): hidden_all = lax.all_gather(hidden, 'grp', axis=0, tiled=True)[send_order]  8.86 us
    slice x3, local copies, waits for them, and re-layouts, shards(): stats = jnp.stack([local_stat[:, :, 0], local_stat[:, :, HD // 2]], axis=0)  8.18 us
    all_to_all x1, blocking collectives, shards(): lax.all_to_all(outgoing, 'grp', split_axis=0, concat_axis=2, tiled=True)  7.31 us
  transfers between devices with their start and end apart: 4, of which 4 were waited for; matrix products, arithmetic and copies ran while one was open for 7% of the time, Pallas kernels for 0%

profile of v2, /device:TPU:0, one launch (start us, length us, event | category | flops | bytes accessed | tf_op | source)
XLA Modules:
  0.0 241.5 jit_solution(17532401085884404227)
XLA Ops:
  1.3 8.9 %all_gather.6 = bf16[256,1024]{1,0:T(8,128)(2,1)S(1)} all-gather(bf16[64,1024]{1,0:T(8,128)(2,1)} %param.10), channel_id=1, replica_groups=mesh['seq'=8,'grp'=4] {'grp'}, dimensions={0}, use_global_device_ids=true | all-gather | bytes 655360 | tf_op jit(solution)/shard_map/all_gather | solution.py:153
  11.3 5.5 %fusion.25 = f32[256,2560]{1,0:T(8,128)} fusion(bf16[256,1024]{1,0:T(8,128)(2,1)S(1)} %gather_fusion.2, bf16[1024,2560]{1,0:T(8,128)(2,1)} %param.11), kind=kOutput, calls=%fused_computation.90 | convolution fusion | flops 1342177280 | bytes 8388608 | tf_op jit(solution)/shard_map/dot_general | solution.py:154
  16.8 6.0 %all-to-all-start = ((f32[8,32,2560]{2,1,0:T(8,128)}), f32[8,32,2560]{2,1,0:T(8,128)S(1)}, u32[]{:S(2)}, u32[]{:S(2)}) async-start(f32[8,32,2560]{2,1,0:T(8,128)} %bitcast.68), calls=%async_computation | async-start | bytes 5242880 | tf_op jit(solution)/shard_map/all_to_all | solution.py:157
  24.3 58.5 %all-to-all-done = f32[8,32,2560]{2,1,0:T(8,128)S(1)} async-done(((f32[8,32,2560]{2,1,0:T(8,128)}), f32[8,32,2560]{2,1,0:T(8,128)S(1)}, u32[]{:S(2)}, u32[]{:S(2)}) %all-to-all-start) | async-done | bytes 2621472 | tf_op jit(solution)/shard_map/all_to_all | solution.py:157
  83.2 1.5 fusion.5
  84.8 7.3 %all_to_all.45 = bf16[4,8,2560]{2,1,0:T(8,128)(2,1)S(1)} all-to-all(bf16[4,8,2560]{2,1,0:T(8,128)(2,1)S(1)} %fusion.5), channel_id=1, replica_groups=mesh['seq'=8,'grp'=4] {'grp'}, dimensions={0} | all-to-all | bytes 327680 | tf_op jit(solution)/shard_map/all_to_all | solution.py:171
  92.3 1.2 broadcast_in_dim.174
  93.5 3.6 %all-to-all-start.2 = ((bf16[8,8,80,128]{3,2,1,0:T(8,128)(2,1)}), bf16[8,8,80,128]{3,2,1,0:T(8,128)(2,1)S(1)}, u32[]{:S(2)}, u32[]{:S(2)}) async-start(bf16[8,8,80,128]{3,2,1,0:T(8,128)(2,1)} %broadcast_in_dim.174), calls=%async_computation.2 | async-start | bytes 2621440 | tf_op jit(solution)/shard_map/all_to_all | solution.py:173
  99.9 28.8 %all-to-all-done.2 = bf16[8,8,80,128]{3,2,1,0:T(8,128)(2,1)S(1)} async-done(((bf16[8,8,80,128]{3,2,1,0:T(8,128)(2,1)}), bf16[8,8,80,128]{3,2,1,0:T(8,128)(2,1)S(1)}, u32[]{:S(2)}, u32[]{:S(2)}) %all-to-all-start.2) | async-done | bytes 1310752 | tf_op jit(solution)/shard_map/all_to_all | solution.py:173
  129.8 20.5 %shard_map.100 = (f32[64,64,128]{2,1,0:T(8,128)}, f32[64,64,128]{2,1,0:T(8,128)}) custom-call(s32[32]{0:T(128)} %get-tuple-element.10.owner_ref, s32[32]{0:T(128)} %get-tuple-element.9.live_ref, bf16[64,80,128]{2,1,0:T(8,128)(2,1)} %bitcast.65, bf16[1,4096,1024]{2,1,0:T(8,128)(2,1)} %key_ref.1, bf16[1,4096,1024]{2,1,0:T(8,128)(2,1)} %value_ref.1), custom_call_target="tpu_custom_call" | custom-call | flops 1073741824 | bytes 16777216 | tf_op jit(solution)/shard_map/pallas_call | solution.py:105
  150.3 4.4 %fusion.24 = (f32[64,64,1]{2,1,0:T(8,128)}, f32[64,64,1]{2,1,0:T(8,128)S(1)}) fusion(f32[64,64,128]{2,1,0:T(8,128)} %get-tuple-element.8), kind=kLoop, calls=%fused_computation.89 | loop fusion | bytes 65536 | tf_op jit(solution)/shard_map/slice | solution.py:221
  154.7 2.6 %copy.45 = f32[64,64,1]{0,1,2:T(8,128)S(1)} copy(f32[64,64,1]{2,1,0:T(8,128)} %get-tuple-element.20) | data formatting | bytes 32768 | tf_op jit(solution)/shard_map/slice | solution.py:221
  159.6 3.6 %all-to-all-start.4 = ((f32[8,1,1024]{2,1,0:T(1,128)}), f32[8,1,1024]{2,1,0:T(1,128)S(1)}, u32[]{:S(2)}, u32[]{:S(2)}) async-start(f32[8,1,1024]{2,1,0:T(1,128)} %all_to_all.38), calls=%async_computation.4 | async-start | bytes 65536 | tf_op jit(solution)/shard_map/all_to_all | solution.py:223
  163.2 1.8 convert_element_type.48
  165.5 1.6 copy.56
  167.1 2.8 %all-to-all-done.4 = f32[8,1,1024]{2,1,0:T(1,128)S(1)} async-done(((f32[8,1,1024]{2,1,0:T(1,128)}), f32[8,1,1024]{2,1,0:T(1,128)S(1)}, u32[]{:S(2)}, u32[]{:S(2)}) %all-to-all-start.4) | async-done | bytes 32800 | tf_op jit(solution)/shard_map/all_to_all | solution.py:223
  169.9 3.7 %all-to-all-start.3 = ((bf16[8,64,1024]{2,1,0:T(8,128)(2,1)}), bf16[8,64,1024]{2,1,0:T(8,128)(2,1)S(1)}, u32[]{:S(2)}, u32[]{:S(2)}) async-start(bf16[8,64,1024]{2,1,0:T(8,128)(2,1)} %bitcast.64), calls=%async_computation.3 | async-start | bytes 2097152 | tf_op jit(solution)/shard_map/all_to_all | solution.py:212
  173.7 1.6 dynamic-slice_convert_fusion
  176.9 2.0 broadcast_in_dim.175
  178.9 1.7 reshape.291
  182.1 16.6 %all-to-all-done.3 = bf16[8,64,1024]{2,1,0:T(8,128)(2,1)S(1)} async-done(((bf16[8,64,1024]{2,1,0:T(8,128)(2,1)}), bf16[8,64,1024]{2,1,0:T(8,128)(2,1)S(1)}, u32[]{:S(2)}, u32[]{:S(2)}) %all-to-all-start.3) | async-done | bytes 1048608 | tf_op jit(solution)/shard_map/all_to_all | solution.py:212
  199.7 6.5 %all_gather.7 = bf16[256,1024]{1,0:T(8,128)(2,1)S(1)} all-gather(bf16[64,1024]{1,0:T(8,128)(2,1)S(1)} %fusion.6), channel_id=1, replica_groups=mesh['seq'=8,'grp'=4] {'grp'}, dimensions={0}, use_global_device_ids=true | all-gather | bytes 655360 | tf_op jit(solution)/shard_map/all_gather | solution.py:244
  207.4 3.4 %convolution_convert_fusion = bf16[256,2048]{1,0:T(8,128)(2,1)S(1)} fusion(bf16[256,1024]{1,0:T(8,128)(2,1)S(1)} %gather_fusion.4, bf16[1024,2048]{1,0:T(8,128)(2,1)} %param.13), kind=kOutput, calls=%fused_computation.5 | convolution fusion | flops 1074266112 | bytes 5767168 | tf_op jit(solution)/shard_map/dot_general | solution.py:246
  210.8 29.9 %all_to_all.46 = bf16[8,32,2048]{2,1,0:T(8,128)(2,1)S(1)} all-to-all(bf16[8,32,2048]{2,1,0:T(8,128)(2,1)S(1)} %bitcast.71), channel_id=1, replica_groups=mesh['seq'=8,'grp'=4] {'seq'}, dimensions={0} | all-to-all | bytes 2097152 | tf_op jit(solution)/shard_map/all_to_all | solution.py:247
  (67 shorter events, 17.0 us)
Async XLA Ops:
  0.0 98.0 %copy-start = (s32[256,128]{1,0:T(8,128)S(1)}, s32[256,128]{1,0:T(8,128)}, u32[]{:S(2)}) copy-start(s32[256,128]{1,0:T(8,128)} %param.17) | copy-start | bytes 393220
  16.8 6.1 %copy-start.5 = (s32[3,256]{1,0:T(4,128)S(1)}, s32[3,256]{1,0:T(4,128)}, u32[]{:S(2)}) copy-start(s32[3,256]{1,0:T(4,128)} %param.18) | copy-start | bytes 9220
  16.8 66.0 %all-to-all-start = ((f32[8,32,2560]{2,1,0:T(8,128)}), f32[8,32,2560]{2,1,0:T(8,128)S(1)}, u32[]{:S(2)}, u32[]{:S(2)}) async-start(f32[8,32,2560]{2,1,0:T(8,128)} %bitcast.68), calls=%async_computation | async-start | bytes 5242880 | tf_op jit(solution)/shard_map/all_to_all | solution.py:157
  22.8 60.1 %copy-start.4 = (f32[2560]{0:T(1024)S(1)}, f32[2560]{0:T(1024)}, u32[]{:S(2)}) copy-start(f32[2560]{0:T(1024)} %param.12) | copy-start | bytes 30724
  92.2 5.0 %copy-start.1 = (s32[256]{0:T(256)S(1)}, s32[256]{0:T(256)}, u32[]{:S(2)}) copy-start(s32[256]{0:T(256)} %param.16) | copy-start | bytes 3076
  93.5 35.3 %all-to-all-start.2 = ((bf16[8,8,80,128]{3,2,1,0:T(8,128)(2,1)}), bf16[8,8,80,128]{3,2,1,0:T(8,128)(2,1)S(1)}, u32[]{:S(2)}, u32[]{:S(2)}) async-start(bf16[8,8,80,128]{3,2,1,0:T(8,128)(2,1)} %broadcast_in_dim.174), calls=%async_computation.2 | async-start | bytes 2621440 | tf_op jit(solution)/shard_map/all_to_all | solution.py:173
  128.7 1.1 copy-start.2
  159.6 10.3 %all-to-all-start.4 = ((f32[8,1,1024]{2,1,0:T(1,128)}), f32[8,1,1024]{2,1,0:T(1,128)S(1)}, u32[]{:S(2)}, u32[]{:S(2)}) async-start(f32[8,1,1024]{2,1,0:T(1,128)} %all_to_all.38), calls=%async_computation.4 | async-start | bytes 65536 | tf_op jit(solution)/shard_map/all_to_all | solution.py:223
  169.9 28.8 %all-to-all-start.3 = ((bf16[8,64,1024]{2,1,0:T(8,128)(2,1)}), bf16[8,64,1024]{2,1,0:T(8,128)(2,1)S(1)}, u32[]{:S(2)}, u32[]{:S(2)}) async-start(bf16[8,64,1024]{2,1,0:T(8,128)(2,1)} %bitcast.64), calls=%async_computation.3 | async-start | bytes 2097152 | tf_op jit(solution)/shard_map/all_to_all | solution.py:212
  198.7 0.8 copy-start.3
